TPU v7x, 32 devices: a whole 2x2x4 slice. The times are simulated.
32 devices in a mesh: seq: 4 (over z), tp: 8 (over y, x, core).
Axes of the slice: x: 2, y: 2, z: 4, core: 2. Of those that a mesh axis runs over, the one named last changes fastest.
Arguments:
- tokens: bfloat16 [2048, 4096], P('seq'), may hold values from -80 to 80
- norm_gain: float32 [4096], replicated, may hold values from 0.1 to 1.9
- query_weight: bfloat16 [4096, 4096], P(None, 'tp'), may hold values from -1 to 1
- key_weight: bfloat16 [4096, 1024], P(None, 'tp'), may hold values from -8 to 8
- value_weight: bfloat16 [4096, 1024], P(None, 'tp'), may hold values from -0.09375 to 0.09375
- out_weight: bfloat16 [4096, 4096], P(None, 'tp'), may hold values from -1 to 1
- segments: int32 [2048], replicated, may hold values from 0 to 2, never falling along the last dimension, each value on 1 to 1024 neighbouring positions
Outputs:
- attn_out: bfloat16 [2048, 4096], P('seq', 'tp')
All inputs are finite; a program needn't handle non-finite values.
Results may differ from a plain program's by a relative error of at most 0.013.
The roundings to bfloat16 on the way count: a program that leaves them out, or rounds other values in their place, can miss the bound.
Values may be sent and summed in bfloat16 or wider, within the bound.
No kernel may reach another device: no remote copies, remote signals or barrier semaphores. Data moves between devices by JAX's collectives and lax.ppermute only.
A program may use at most 128 MiB of HBM per device.

v0:
```python
import functools
import math

import jax
import jax.numpy as jnp
import numpy as np
from jax import lax
from jax.experimental import pallas as pl
from jax.experimental.pallas import tpu as pltpu
from jax.sharding import PartitionSpec as P

HEAD_DIM = 128
WINDOW = 4096
EPSILON = 1e-05
BASE = 10000.0


VMEM = pl.BlockSpec(memory_space=pltpu.VMEM)
HBM = pl.BlockSpec(memory_space=pltpu.HBM)
PARAMS = pltpu.CompilerParams(vmem_limit_bytes=16 << 20)


def in_hbm(*arrays):
    return [pltpu.with_memory_space_constraint(a, pltpu.HBM) for a in arrays]


STEP = 16


def rotation_tables(block_rows, blocks):
    freqs = BASE ** (-2.0 * (np.arange(HEAD_DIM) % (HEAD_DIM // 2)) / HEAD_DIM)
    coarse = np.arange(0, block_rows * blocks, STEP)[:, None] * freqs
    fine = np.arange(STEP)[:, None] * freqs
    tables = (np.cos(coarse), np.sin(coarse), np.cos(fine), np.sin(fine))
    return [jnp.asarray(t, jnp.float32) for t in tables]


def rotate(x, cosine, sine):
    return (x * cosine + pltpu.roll(x, HEAD_DIM // 2, 1) * sine).astype(jnp.bfloat16)


def heads_of(width):
    return [slice(h, h + HEAD_DIM) for h in range(0, width, HEAD_DIM)]


def normalise(tokens, gain):
    wide = tokens.astype(jnp.float32)
    scale = lax.rsqrt(jnp.mean(wide * wide, axis=-1, keepdims=True) + EPSILON)
    return (wide * scale * gain).astype(jnp.bfloat16)


def key_value_of(normed, weight, cosine, sine, kv_ref, here):
    product = jnp.dot(normed, weight, preferred_element_type=jnp.float32)
    width = kv_ref.shape[1] // 2
    for h in heads_of(width):
        kv_ref[here, h] = rotate(product[:, h], cosine, sine)
    kv_ref[here, width:] = product[:, width:].astype(jnp.bfloat16)


def second_half_kernel(
    tile, tokens, gain, key_weight, value_weight, coarse_cos, coarse_sin, fine_cos, fine_sin, segments,
    kv_ref, normed_ref, weight, first_tokens, gain_copy, cosine, sine, limits,
    held, coarse_c, coarse_s, fine_c, fine_s, numbers, tile_sems, sems,
):
    rows, width = kv_ref.shape[0], key_weight.shape[1]
    steps = rows // tile
    tiles = [
        pltpu.make_async_copy(
            tokens.at[rows + i * tile : rows + (i + 1) * tile, :],
            held.at[i * tile : (i + 1) * tile, :],
            tile_sems.at[i],
        )
        for i in range(steps)
    ]
    groups = cosine.shape[0] // STEP
    coarse = pl.ds(pl.multiple_of(lax.axis_index("seq") * groups, groups), groups)
    moves = [
        (gain, gain_copy),
        (key_weight, weight.at[:, :width]),
        (value_weight, weight.at[:, width:]),
        (coarse_cos.at[coarse, :], coarse_c),
        (coarse_sin.at[coarse, :], coarse_s),
        (fine_cos, fine_c),
        (fine_sin, fine_s),
        (tokens.at[:rows, :], first_tokens),
        (segments, numbers),
    ]
    moves = [pltpu.make_async_copy(a, b, sems.at[i]) for i, (a, b) in enumerate(moves)]
    for move in [moves[8], moves[0]] + tiles[:2] + moves[3:7] + tiles[2:] + moves[1:3] + moves[7:8]:
        move.start()
    moves[8].wait()
    for value in (1, 2):
        before = jnp.sum((numbers[...] < value).astype(jnp.float32), axis=0, keepdims=True)
        count = jnp.broadcast_to(jnp.sum(before, axis=1, keepdims=True), before.shape)
        limits[value - 1 : value, :] = count.astype(jnp.int32)
    moves[0].wait()
    for i in range(steps):
        here = slice(i * tile, (i + 1) * tile)
        tiles[i].wait()
        normed_ref[here, :] = normalise(held[here, :], gain_copy[...])
    for move in moves[3:7]:
        move.wait()
    cos_f, sin_f = fine_c[...], fine_s[...]
    lane = lax.broadcasted_iota(jnp.int32, cos_f.shape, 1)
    for group in range(groups):
        cos_g, sin_g = coarse_c[group : group + 1, :], coarse_s[group : group + 1, :]
        turned = sin_g * cos_f + cos_g * sin_f
        here = slice(group * STEP, (group + 1) * STEP)
        cosine[here, :] = cos_g * cos_f - sin_g * sin_f
        sine[here, :] = jnp.where(lane < HEAD_DIM // 2, -turned, turned)
    moves[1].wait()
    moves[2].wait()
    key_value_of(normed_ref[...], weight[...], cosine[rows:, :], sine[rows:, :], kv_ref, slice(None))
    moves[7].wait()


def second_half(tokens, gain, key_weight, value_weight, tables, segments):
    block_rows, depth = tokens.shape
    half, width = block_rows // 2, key_weight.shape[1]
    tile = min(half, 32)
    shape, bf16, f32 = jax.ShapeDtypeStruct, jnp.bfloat16, jnp.float32
    return pl.pallas_call(
        functools.partial(second_half_kernel, tile),
        out_shape=(
            shape((half, 2 * width), bf16),
            shape((half, depth), bf16),
            shape((depth, 2 * width), bf16),
            shape((half, depth), bf16),
            shape(gain.shape, f32),
            shape((block_rows, HEAD_DIM), f32),
            shape((block_rows, HEAD_DIM), f32),
            shape((2, HEAD_DIM), jnp.int32),
        ),
        in_specs=[HBM] * 9,
        out_specs=(VMEM,) * 8,
        scratch_shapes=[pltpu.VMEM((half, depth), bf16)]
        + [pltpu.VMEM((block_rows // STEP, HEAD_DIM), f32)] * 2
        + [pltpu.VMEM((STEP, HEAD_DIM), f32)] * 2
        + [pltpu.VMEM(segments.shape, jnp.int32)]
        + [pltpu.SemaphoreType.DMA((half // tile,)), pltpu.SemaphoreType.DMA((9,))],
        compiler_params=PARAMS,
        name="second_half",
    )(*in_hbm(tokens, gain, key_weight, value_weight, *tables, segments))


def first_half_kernel(tokens, gain, weight, cosine, sine, kv_ref, normed_ref):
    rows = kv_ref.shape[0]
    normed_ref[...] = normalise(tokens[...], gain[...])
    key_value_of(normed_ref[...], weight[...], cosine[:rows, :], sine[:rows, :], kv_ref, slice(None))


def first_half(tokens, gain, weight, cosine, sine):
    half = tokens.shape[0]
    return pl.pallas_call(
        first_half_kernel,
        out_shape=(
            jax.ShapeDtypeStruct((half, weight.shape[1]), jnp.bfloat16),
            jax.ShapeDtypeStruct(tokens.shape, jnp.bfloat16),
        ),
        in_specs=[VMEM] * 5,
        out_specs=(VMEM,) * 2,
        compiler_params=PARAMS,
        name="first_half",
    )(tokens, gain, weight, cosine, sine)


def query_kernel(part, normed, weight, cosine, sine, out_ref):
    rows = slice(part * normed.shape[0], (part + 1) * normed.shape[0])
    product = jnp.dot(normed[...], weight[...], preferred_element_type=jnp.float32)
    for h in heads_of(weight.shape[1]):
        out_ref[:, h] = rotate(product[:, h], cosine[rows, :], sine[rows, :])


def query(part, normed, weight, cosine, sine):
    return pl.pallas_call(
        functools.partial(query_kernel, part),
        out_shape=jax.ShapeDtypeStruct((normed.shape[0], weight.shape[1]), jnp.bfloat16),
        in_specs=[VMEM] * 4,
        out_specs=VMEM,
        compiler_params=PARAMS,
    )(normed, weight, cosine, sine)


AHEAD = 3
FACTOR = math.log2(math.e) / math.sqrt(HEAD_DIM)


def bias_of(part, place, back, half, limits, bias_ref, column):
    base = (2 * lax.axis_index("seq") + part) * half
    row = base + lax.broadcasted_iota(jnp.int32, (half, HEAD_DIM), 0)
    starts = [jnp.broadcast_to(limits[i : i + 1, :], row.shape) for i in range(2)]
    start = jnp.where(row >= starts[1], starts[1], jnp.where(row >= starts[0], starts[0], 0))
    start = jnp.maximum(start, row - (WINDOW - 1))
    first = base - (back - place) * half
    for left in range(0, half, HEAD_DIM):
        key = first + left + lax.broadcasted_iota(jnp.int32, (half, HEAD_DIM), 1)
        mask = key >= start
        if place == back:
            mask = mask & (key <= row)
        bias_ref[:, column + left : column + left + HEAD_DIM] = jnp.where(
            mask, jnp.float32(0), jnp.float32(-1e30)
        )


def attend_kernel(part, back, places, early, late, limits, q_ref, *refs):
    kv_refs, refs = refs[: len(places)], refs[len(places) :]
    bias_ref = refs[-1]
    outs = 2 if late else 0
    half = q_ref.shape[0]
    kv_width = kv_refs[0].shape[1] // 2
    group = q_ref.shape[1] // kv_width
    for i, place in enumerate(places):
        bias_of(part, place, back, half, limits, bias_ref, i * half)
    ones = jnp.ones((half, HEAD_DIM), jnp.bfloat16)
    tile = half
    wide = half // HEAD_DIM

    def score(h, rows):
        first = (h // group) * HEAD_DIM
        q = q_ref[rows, h * HEAD_DIM : (h + 1) * HEAD_DIM]
        scores = []
        for i, kv in enumerate(kv_refs):
            s = lax.dot_general(
                q, kv[:, first : first + HEAD_DIM], (((1,), (1,)), ((), ())), preferred_element_type=jnp.float32
            )
            scores.append(s * FACTOR + bias_ref[rows, i * half : (i + 1) * half])
        return scores

    def finish(h, rows, scores):
        first = kv_width + (h // group) * HEAD_DIM
        head = slice(h * HEAD_DIM, (h + 1) * HEAD_DIM)
        pair = slice(2 * h * HEAD_DIM, 2 * (h + 1) * HEAD_DIM)
        top = functools.reduce(jnp.maximum, scores)
        top = functools.reduce(jnp.maximum, [top[:, c * HEAD_DIM : (c + 1) * HEAD_DIM] for c in range(wide)])
        peak = jnp.broadcast_to(jnp.max(top, axis=-1, keepdims=True), top.shape)
        summed = 0.0
        if late:
            before = refs[1][rows, head]
            peak = jnp.maximum(peak, before)
            fade = jnp.exp2(before - peak)
            summed = refs[0][rows, pair] * jnp.concatenate([fade, fade], axis=1)
        peaks = jnp.concatenate([peak] * wide, axis=1)
        for s, kv in zip(scores, kv_refs):
            w = jnp.exp2(s - peaks).astype(jnp.bfloat16)
            both = jnp.concatenate([kv[:, first : first + HEAD_DIM], ones], axis=1)
            summed = summed + jnp.dot(w, both, preferred_element_type=jnp.float32)
        if early:
            refs[0][rows, pair] = summed
            refs[1][rows, head] = peak
        else:
            result = (summed[:, :HEAD_DIM] / summed[:, HEAD_DIM:]).astype(jnp.bfloat16)
            refs[outs][rows, head] = result
            for i, piece in enumerate(refs[outs + 1 : -1]):
                piece[:, head] = result[i * piece.shape[0] : (i + 1) * piece.shape[0], :]

    units = [
        (h, slice(row, row + tile)) for h in range(q_ref.shape[1] // HEAD_DIM) for row in range(0, half, tile)
    ]
    waiting = []
    for unit in units:
        waiting.append((*unit, score(*unit)))
        if len(waiting) > AHEAD:
            finish(*waiting.pop(0))
    for unit in waiting:
        finish(*unit)


def attend(part, back, places, queries, limits, key_values, early=False, before=(), pieces=0):
    half, width = queries.shape
    if early:
        shape = (
            jax.ShapeDtypeStruct((half, 2 * width), jnp.float32),
            jax.ShapeDtypeStruct((half, width), jnp.float32),
        )
    else:
        shape = [jax.ShapeDtypeStruct((half, width), jnp.bfloat16)]
        shape += [jax.ShapeDtypeStruct((half // max(pieces, 1), width), jnp.bfloat16)] * pieces
    key_values = [key_values[p] for p in places]
    return pl.pallas_call(
        functools.partial(attend_kernel, part, back, tuple(places), early, bool(before)),
        out_shape=shape,
        in_specs=[VMEM] * (2 + len(places) + len(before)),
        out_specs=[VMEM] * len(shape),
        scratch_shapes=[pltpu.VMEM((half, len(places) * half), jnp.float32)],
        compiler_params=pltpu.CompilerParams(vmem_limit_bytes=max(16, 2 * len(places)) << 20),
    )(limits, queries, *key_values, *before)


def added(bits, total, weight, pieces):
    depth = pieces[0][0].shape[1]
    me = lax.axis_index("tp")
    for bit, piece in zip(bits, pieces):
        owner = jnp.bitwise_xor(me, bit)
        rows = pl.ds(pl.multiple_of(owner * depth, depth), depth)
        x = jnp.concatenate([a[...] for a in piece], axis=0) if len(piece) > 1 else piece[0][...]
        total = total + jnp.dot(x, weight[rows, :], preferred_element_type=jnp.float32)
    return total


def grouped(refs, counts):
    groups, place = [], 0
    for count in counts:
        groups.append(refs[place : place + count])
        place += count
    return groups, refs[place:]


def product_kernel(bits, counts, weight, *refs):
    pieces, rest = grouped(refs, counts)
    rest[-1][...] = added(bits, rest[0][...] if len(rest) > 1 else 0.0, weight, pieces)


def product(weight, got, total=None):
    bits, pieces = zip(*got)
    counts = [len(piece) for piece in pieces]
    xs = [a for piece in pieces for a in piece]
    extra = () if total is None else (total,)
    return pl.pallas_call(
        functools.partial(product_kernel, bits, counts),
        out_shape=jax.ShapeDtypeStruct((sum(a.shape[0] for a in pieces[0]), weight.shape[1]), jnp.float32),
        in_specs=[VMEM] * (1 + len(xs) + len(extra)),
        out_specs=VMEM,
        compiler_params=PARAMS,
    )(weight, *xs, *extra)


def store_kernel(bits, counts, weight, *refs):
    pieces, rest = grouped(refs, counts)
    totals, (out_ref, rounded, sems) = rest[:2], rest[2:]
    half = totals[0].shape[0]
    moves = []
    for part in (1, 0):
        rows = slice(part * half, (part + 1) * half)
        rounded[rows, :] = added(bits[part], totals[part][...], weight, [pieces[part]]).astype(rounded.dtype)
        moves.append(pltpu.make_async_copy(rounded.at[rows, :], out_ref.at[rows, :], sems.at[part]))
        moves[-1].start()
    for move in moves:
        move.wait()


def store(weight, bits, pieces, totals):
    xs = [a for piece in pieces for a in piece]
    half, width = totals[0].shape
    return pl.pallas_call(
        functools.partial(store_kernel, [(bits,)] * 2, [len(piece) for piece in pieces]),
        out_shape=pltpu.HBM((2 * half, width), jnp.bfloat16),
        in_specs=[VMEM] * (3 + len(xs)),
        out_specs=HBM,
        scratch_shapes=[pltpu.VMEM((2 * half, width), jnp.bfloat16), pltpu.SemaphoreType.DMA((2,))],
        compiler_params=PARAMS,
        name="store",
    )(weight, *xs, *totals)


def shards(tokens, norm_gain, query_weight, key_weight, value_weight, out_weight, segments):
    block_rows = tokens.shape[0]
    half = block_rows // 2
    seq_count, tp_count = lax.axis_size("seq"), lax.axis_size("tp")
    total = block_rows * seq_count
    reach = min(WINDOW, total // 2)
    back = min((reach - 2) // half + 1, 2 * seq_count - 1)

    def onward(hop):
        pairs = [(i, i + 1, 0) for i in range(hop - 1, seq_count - 1)]
        pairs = pairs + [(seq_count - 1, hop - 1, 0)] + [(i, i, 1) for i in range(hop - 1)]
        return [(a * tp_count + t, b * tp_count + (t ^ c)) for a, b, c in pairs for t in range(tp_count)]


    halves, normed, queries = [None] * (back + 2), [None, None], [None, None]
    halves[0], normed[1], weight, first_tokens, gain, cosine, sine, limits = second_half(
        tokens,
        norm_gain[None, :],
        key_weight,
        value_weight,
        rotation_tables(block_rows, seq_count),
        segments.reshape(-1, HEAD_DIM),
    )
    halves[1], normed[0] = first_half(first_tokens, gain, weight, cosine, sine)
    for distance in range(2, back + 2):
        halves[distance] = lax.ppermute(halves[distance - 2], ("seq", "tp"), onward(distance // 2))
    for part in (1, 0):
        queries[part] = query(part, normed[part], query_weight, cosine, sine)

    def swap(x, bit):
        return lax.ppermute(x, "tp", [(i, i ^ bit) for i in range(tp_count)])

    got, totals = {}, [None, None]
    for part in (1, 0):
        key_values = halves[1 - part : 1 - part + back + 1][::-1]
        if part == 1:
            before = attend(part, back, range(back - 2, back + 1), queries[part], limits, key_values, early=True)
            (mine,) = attend(part, back, range(back - 2), queries[part], limits, key_values, before=before)
        else:
            mine, *pair = attend(part, back, range(back + 1), queries[part], limits, key_values, pieces=2)
        if part == 1:
            x, y = swap(mine, 2), swap(mine, 4)
            has = {0: (mine,), 2: (x,), 4: (y,), 6: (swap(x, 4),)}
        else:
            y = [swap(a, 4) for a in pair]
            x = swap(mine, 2)
            has = {0: (mine,), 2: (x,), 4: tuple(y), 6: tuple(swap(a, 2) for a in y)}
        for bits in (0, 2, 4, 6):
            has[bits | 1] = tuple(swap(a, 1) for a in has[bits])
        got[part] = has
    for part in (1, 0):
        pieces = lambda *bits: [(b, got[part][b]) for b in bits]
        acc = None
        for bits in ((0, 1), (2, 3, 4, 5), (6,)):
            acc = product(out_weight, pieces(*bits), acc)
        totals[part] = acc
    return store(out_weight, 7, [got[part][7] for part in (0, 1)], totals)


def solution(mesh):
    return jax.shard_map(
        shards,
        mesh=mesh,
        in_specs=(P("seq", None), P(), P(None, "tp"), P(None, "tp"), P(None, "tp"), P(None, "tp"), P()),
        out_specs=P("seq", "tp"),
        check_vma=False,
    )
```

profile of v0, /device:TPU:9, one launch (start us, length us, event | category | flops | bytes accessed | tf_op | source)
XLA Modules:
  0.0 55.1 jit_solution(18290375495218946279)
XLA Ops:
  0.0 3.4 %second_half.1 = (bf16[256,256]{1,0:T(8,128)(2,1)S(1)}, bf16[256,4096]{1,0:T(8,128)(2,1)S(1)}, bf16[4096,256]{1,0:T(8,128)(2,1)S(1)}, bf16[256,4096]{1,0:T(8,128...) custom-call(bf16[512,4096]{1,0:T(8,128)(2,1)} %tokens.1, ...), custom_call_target="tpu_custom_call" | custom-call | tf_op jit(solution)/shard_map/second_half/pallas_call | solution.py:122
  3.4 0.0 copy-start.1
  3.4 1.4 %first_half.1 = (bf16[256,256]{1,0:T(8,128)(2,1)S(1)}, bf16[256,4096]{1,0:T(8,128)(2,1)S(1)}) custom-call(bf16[256,4096]{1,0:T(8,128)(2,1)S(1)} %get-tuple-element.21.tokens, f32[1,4096]{1,0:T(1,128)S(1)} %get-tuple-element.22.gain, bf16[4096,256]{1,0:T(8,128)(2,1)S(1)} %get-tuple-element.23.weight, f32[512,128]{1,0:T(8,128)S(1)} %get-tuple-element.24.cosine, ...), custom_call_target="tpu_custom_call" | custom-call | tf_op jit(solution)/shard_map/first_half/pallas_call | solution.py:154
  4.8 1.3 %collective-permute-start = (bf16[256,256]{1,0:T(8,128)(2,1)S(1)}, bf16[256,256]{1,0:T(8,128)(2,1)S(1)}, u32[]{:S(2)}, u32[]{:S(2)}) collective-permute-start(bf16[256,256]{1,0:T(8,128)(2,1)S(1)} %get-tuple-element.27.refs_4_.refs_1_), channel_id=1, source_target_pairs={{0,8},{1,9},{2,10},{3,11},{4,12},{5,13},{6,14},{7,15},{8,16},{9,17... | collective-permute-start | bytes 393224 | tf_op jit(solution)/shard_map/ppermute | solution.py:380
  6.2 1.3 %collective-permute-start.2 = (bf16[256,256]{1,0:T(8,128)(2,1)S(1)}, bf16[256,256]{1,0:T(8,128)(2,1)S(1)}, u32[]{:S(2)}, u32[]{:S(2)}) collective-permute-start(bf16[256,256]{1,0:T(8,128)(2,1)S(1)} %get-tuple-element.28.refs_2_), channel_id=1, source_target_pairs={{0,8},{1,9},{2,10},{3,11},{4,12},{5,13},{6,14},{7,15},{8,16},{9,17... | collective-permute-start | bytes 393224 | tf_op jit(solution)/shard_map/ppermute | solution.py:380
  7.5 1.8 %collective-permute-done.refs_2_.refs_1_ = bf16[256,256]{1,0:T(8,128)(2,1)S(1)} collective-permute-done((bf16[256,256]{1,0:T(8,128)(2,1)S(1)}, bf16[256,256]{1,0:T(8,128)(2,1)S(1)}, u32[]{:S(2)}, u32[]{:S(2)}) %collective-permute-start) | collective-permute-done | bytes 131104 | tf_op jit(solution)/shard_map/ppermute | solution.py:380
  9.3 1.3 %collective-permute-start.1 = (bf16[256,256]{1,0:T(8,128)(2,1)S(1)}, bf16[256,256]{1,0:T(8,128)(2,1)S(1)}, u32[]{:S(2)}, u32[]{:S(2)}) collective-permute-start(bf16[256,256]{1,0:T(8,128)(2,1)S(1)} %collective-permute-done.refs_2_.refs_1_), channel_id=1, source_target_pairs={{8,16},{9,17},{10,18},{11,19},{12,20},{13,21},{14,22},{15,23},{16,... | collective-permute-start | bytes 393224 | tf_op jit(solution)/shard_map/ppermute | solution.py:380
  10.6 1.5 %collective-permute-done.2.refs_3_.refs_0_ = bf16[256,256]{1,0:T(8,128)(2,1)S(1)} collective-permute-done((bf16[256,256]{1,0:T(8,128)(2,1)S(1)}, bf16[256,256]{1,0:T(8,128)(2,1)S(1)}, u32[]{:S(2)}, u32[]{:S(2)}) %collective-permute-start.2) | collective-permute-done | bytes 131104 | tf_op jit(solution)/shard_map/ppermute | solution.py:380
  12.1 1.3 %collective-permute-start.3 = (bf16[256,256]{1,0:T(8,128)(2,1)S(1)}, bf16[256,256]{1,0:T(8,128)(2,1)S(1)}, u32[]{:S(2)}, u32[]{:S(2)}) collective-permute-start(bf16[256,256]{1,0:T(8,128)(2,1)S(1)} %collective-permute-done.2.refs_3_.refs_0_), channel_id=1, source_target_pairs={{8,16},{9,17},{10,18},{11,19},{12,20},{13,21},{14,22},{15,23},{16,... | collective-permute-start | bytes 393224 | tf_op jit(solution)/shard_map/ppermute | solution.py:380
  13.4 0.0 copy-done.1
  13.4 1.4 %shard_map.109.q_ref = bf16[256,512]{1,0:T(8,128)(2,1)S(1)} custom-call(bf16[256,4096]{1,0:T(8,128)(2,1)S(1)} %get-tuple-element.26.normed, bf16[4096,512]{1,0:T(8,128)(2,1)S(1)} %copy-done.1, f32[512,128]{1,0:T(8,128)S(1)} %get-tuple-element.24.cosine, f32[512,128]{1,0:T(8,128)S(1)} %get-tuple-element.25.sine), custom_call_target="tpu_custom_call" | custom-call | tf_op jit(solution)/shard_map/pallas_call | solution.py:175
  14.8 0.4 collective-permute-done.1.refs_0_
  15.2 3.0 %collective-permute-done.3.refs_1_.refs_0_ = bf16[256,256]{1,0:T(8,128)(2,1)S(1)} collective-permute-done((bf16[256,256]{1,0:T(8,128)(2,1)S(1)}, bf16[256,256]{1,0:T(8,128)(2,1)S(1)}, u32[]{:S(2)}, u32[]{:S(2)}) %collective-permute-start.3) | collective-permute-done | bytes 131104 | tf_op jit(solution)/shard_map/ppermute | solution.py:380
  18.2 2.1 %shard_map.110 = (bf16[256,512]{1,0:T(8,128)(2,1)S(1)}, bf16[128,512]{1,0:T(8,128)(2,1)S(1)}, bf16[128,512]{1,0:T(8,128)(2,1)S(1)}) custom-call(s32[2,128]{1,0:T(2,128)S(1)} %get-tuple-element.20.limits, bf16[256,512]{1,0:T(8,128)(2,1)S(1)} %shard_map.109.q_ref, bf16[256,256]{1,0:T(8,128)(2,1)S(1)} %collective-permute-done.1.refs_0_, ...), custom_call_target="tpu_custom_call" | custom-call | tf_op jit(solution)/shard_map/pallas_call | solution.py:279
  20.3 1.3 %collective-permute-start.4 = (bf16[128,512]{1,0:T(8,128)(2,1)S(1)}, bf16[128,512]{1,0:T(8,128)(2,1)S(1)}, u32[]{:S(2)}, u32[]{:S(2)}) collective-permute-start(bf16[128,512]{1,0:T(8,128)(2,1)S(1)} %get-tuple-element.29), channel_id=1, source_target_pairs={{0,4},{1,5},{2,6},{3,7},{4,0},{5,1},{6,2},{7,3},{8,12},{9,13},{10,... | collective-permute-start | bytes 393224 | tf_op jit(solution)/shard_map/ppermute | solution.py:385
  21.5 0.2 collective-permute-start.7
  21.8 0.0 copy-start
  21.8 1.4 %shard_map.111.q_ref = bf16[256,512]{1,0:T(8,128)(2,1)S(1)} custom-call(bf16[256,4096]{1,0:T(8,128)(2,1)S(1)} %get-tuple-element.31.normed, bf16[4096,512]{1,0:T(8,128)(2,1)S(1)} %copy-done.1, f32[512,128]{1,0:T(8,128)S(1)} %get-tuple-element.24.cosine, f32[512,128]{1,0:T(8,128)S(1)} %get-tuple-element.25.sine), custom_call_target="tpu_custom_call" | custom-call | tf_op jit(solution)/shard_map/pallas_call | solution.py:175
  23.2 1.4 %shard_map.112 = (f32[256,1024]{1,0:T(8,128)S(1)}, f32[256,512]{1,0:T(8,128)S(1)}) custom-call(s32[2,128]{1,0:T(2,128)S(1)} %get-tuple-element.20.limits, bf16[256,512]{1,0:T(8,128)(2,1)S(1)} %shard_map.111.q_ref, bf16[256,256]{1,0:T(8,128)(2,1)S(1)} %collective-permute-done.2.refs_3_.refs_0_, bf16[256,256]{1,0:T(8,128)(2,1)S(1)} %get-tuple-element.27.refs_4_.refs_1_, ...), custom_call_target="tpu_custom_call" | custom-call | tf_op jit(solution)/shard_map/pallas_call | solution.py:279
  24.5 1.1 %shard_map.113.refs_0_ = bf16[256,512]{1,0:T(8,128)(2,1)S(1)} custom-call(s32[2,128]{1,0:T(2,128)S(1)} %get-tuple-element.20.limits, bf16[256,512]{1,0:T(8,128)(2,1)S(1)} %shard_map.111.q_ref, bf16[256,256]{1,0:T(8,128)(2,1)S(1)} %collective-permute-done.3.refs_1_.refs_0_, bf16[256,256]{1,0:T(8,128)(2,1)S(1)} %collective-permute-done.refs_2_.refs_1_, ...), custom_call_target="tpu_custom_call" | custom-call | tf_op jit(solution)/shard_map/pallas_call | solution.py:279
  25.6 1.3 %collective-permute-start.10 = (bf16[256,512]{1,0:T(8,128)(2,1)S(1)}, bf16[256,512]{1,0:T(8,128)(2,1)S(1)}, u32[]{:S(2)}, u32[]{:S(2)}) collective-permute-start(bf16[256,512]{1,0:T(8,128)(2,1)S(1)} %shard_map.113.refs_0_), channel_id=1, source_target_pairs={{0,2},{1,3},{2,0},{3,1},{4,6},{5,7},{6,4},{7,5},{8,10},{9,11},{10,... | collective-permute-start | bytes 786440 | tf_op jit(solution)/shard_map/ppermute | solution.py:385
  26.9 0.0 collective-permute-done.4.refs_2_
  26.9 3.0 %collective-permute-start.15 = (bf16[128,512]{1,0:T(8,128)(2,1)S(1)}, bf16[128,512]{1,0:T(8,128)(2,1)S(1)}, u32[]{:S(2)}, u32[]{:S(2)}) collective-permute-start(bf16[128,512]{1,0:T(8,128)(2,1)S(1)} %collective-permute-done.4.refs_2_), channel_id=1, source_target_pairs={{0,1},{1,0},{2,3},{3,2},{4,5},{5,4},{6,7},{7,6},{8,9},{9,8},{10,11... | collective-permute-start | bytes 393224 | tf_op jit(solution)/shard_map/ppermute | solution.py:385
  29.9 0.2 collective-permute-start.5
  30.1 0.0 collective-permute-done.7.refs_3_
  30.1 0.3 collective-permute-start.16
  30.4 1.2 %collective-permute-start.13 = (bf16[256,512]{1,0:T(8,128)(2,1)S(1)}, bf16[256,512]{1,0:T(8,128)(2,1)S(1)}, u32[]{:S(2)}, u32[]{:S(2)}) collective-permute-start(bf16[256,512]{1,0:T(8,128)(2,1)S(1)} %get-tuple-element.34.refs_0_), channel_id=1, source_target_pairs={{0,2},{1,3},{2,0},{3,1},{4,6},{5,7},{6,4},{7,5},{8,10},{9,11},{10,... | collective-permute-start | bytes 786440 | tf_op jit(solution)/shard_map/ppermute | solution.py:385
  31.6 0.0 collective-permute-done.15.refs_4_
  31.6 1.2 %collective-permute-start.19 = (bf16[256,512]{1,0:T(8,128)(2,1)S(1)}, bf16[256,512]{1,0:T(8,128)(2,1)S(1)}, u32[]{:S(2)}, u32[]{:S(2)}) collective-permute-start(bf16[256,512]{1,0:T(8,128)(2,1)S(1)} %shard_map.113.refs_0_), channel_id=1, source_target_pairs={{0,4},{1,5},{2,6},{3,7},{4,0},{5,1},{6,2},{7,3},{8,12},{9,13},{10,... | collective-permute-start | bytes 786440 | tf_op jit(solution)/shard_map/ppermute | solution.py:385
  32.9 2.5 %collective-permute-done.5.refs_0_ = bf16[128,512]{1,0:T(8,128)(2,1)S(1)} collective-permute-done((bf16[128,512]{1,0:T(8,128)(2,1)S(1)}, bf16[128,512]{1,0:T(8,128)(2,1)S(1)}, u32[]{:S(2)}, u32[]{:S(2)}) %collective-permute-start.5) | collective-permute-done | bytes 131104 | tf_op jit(solution)/shard_map/ppermute | solution.py:385
  35.4 3.9 %collective-permute-start.17 = (bf16[256,512]{1,0:T(8,128)(2,1)S(1)}, bf16[256,512]{1,0:T(8,128)(2,1)S(1)}, u32[]{:S(2)}, u32[]{:S(2)}) collective-permute-start(bf16[256,512]{1,0:T(8,128)(2,1)S(1)} %get-tuple-element.34.refs_0_), channel_id=1, source_target_pairs={{0,1},{1,0},{2,3},{3,2},{4,5},{5,4},{6,7},{7,6},{8,9},{9,8},{10,11... | collective-permute-start | bytes 786440 | tf_op jit(solution)/shard_map/ppermute | solution.py:385
  39.3 0.0 collective-permute-done.16.refs_5_
  39.3 2.2 %collective-permute-start.8 = (bf16[128,512]{1,0:T(8,128)(2,1)S(1)}, bf16[128,512]{1,0:T(8,128)(2,1)S(1)}, u32[]{:S(2)}, u32[]{:S(2)}) collective-permute-start(bf16[128,512]{1,0:T(8,128)(2,1)S(1)} %collective-permute-done.7.refs_3_), channel_id=1, source_target_pairs={{0,2},{1,3},{2,0},{3,1},{4,6},{5,7},{6,4},{7,5},{8,10},{9,11},{10,... | collective-permute-start | bytes 393224 | tf_op jit(solution)/shard_map/ppermute | solution.py:385
  41.5 0.0 collective-permute-done.10.refs_0_
  41.5 1.2 %collective-permute-start.11 = (bf16[256,512]{1,0:T(8,128)(2,1)S(1)}, bf16[256,512]{1,0:T(8,128)(2,1)S(1)}, u32[]{:S(2)}, u32[]{:S(2)}) collective-permute-start(bf16[256,512]{1,0:T(8,128)(2,1)S(1)} %collective-permute-done.10.refs_0_), channel_id=1, source_target_pairs={{0,4},{1,5},{2,6},{3,7},{4,0},{5,1},{6,2},{7,3},{8,12},{9,13},{10,... | collective-permute-start | bytes 786440 | tf_op jit(solution)/shard_map/ppermute | solution.py:385
  42.7 2.7 %collective-permute-done.8.refs_1_ = bf16[128,512]{1,0:T(8,128)(2,1)S(1)} collective-permute-done((bf16[128,512]{1,0:T(8,128)(2,1)S(1)}, bf16[128,512]{1,0:T(8,128)(2,1)S(1)}, u32[]{:S(2)}, u32[]{:S(2)}) %collective-permute-start.8) | collective-permute-done | bytes 131104 | tf_op jit(solution)/shard_map/ppermute | solution.py:385
  45.4 0.6 %collective-permute-start.21 = (bf16[256,512]{1,0:T(8,128)(2,1)S(1)}, bf16[256,512]{1,0:T(8,128)(2,1)S(1)}, u32[]{:S(2)}, u32[]{:S(2)}) collective-permute-start(bf16[256,512]{1,0:T(8,128)(2,1)S(1)} %shard_map.113.refs_0_), channel_id=1, source_target_pairs={{0,1},{1,0},{2,3},{3,2},{4,5},{5,4},{6,7},{7,6},{8,9},{9,8},{10,11... | collective-permute-start | bytes 786440 | tf_op jit(solution)/shard_map/ppermute | solution.py:385
  46.0 0.0 collective-permute-done.13.refs_0_
  46.0 0.0 collective-permute-start.14
  46.0 0.0 collective-permute-done.19.refs_2_
  46.0 0.5 collective-permute-start.20
  46.5 0.0 collective-permute-done.17.refs_1_
  46.5 0.1 collective-permute-start.18
  46.6 2.5 %collective-permute-done.11.refs_0_ = bf16[256,512]{1,0:T(8,128)(2,1)S(1)} collective-permute-done((bf16[256,512]{1,0:T(8,128)(2,1)S(1)}, bf16[256,512]{1,0:T(8,128)(2,1)S(1)}, u32[]{:S(2)}, u32[]{:S(2)}) %collective-permute-start.11) | collective-permute-done | bytes 262176 | tf_op jit(solution)/shard_map/ppermute | solution.py:385
  49.1 1.1 %collective-permute-start.12 = (bf16[256,512]{1,0:T(8,128)(2,1)S(1)}, bf16[256,512]{1,0:T(8,128)(2,1)S(1)}, u32[]{:S(2)}, u32[]{:S(2)}) collective-permute-start(bf16[256,512]{1,0:T(8,128)(2,1)S(1)} %collective-permute-done.11.refs_0_), channel_id=1, source_target_pairs={{0,1},{1,0},{2,3},{3,2},{4,5},{5,4},{6,7},{7,6},{8,9},{9,8},{10,11... | collective-permute-start | bytes 786440 | tf_op jit(solution)/shard_map/ppermute | solution.py:385
  50.2 0.0 collective-permute-done.21.refs_1_
  50.2 0.0 collective-permute-start.6
  50.2 0.0 collective-permute-done.14.refs_1_
  50.2 0.5 collective-permute-start.9
  50.7 0.0 copy-done
  50.7 0.4 shard_map.114.refs_6_
  51.2 0.4 shard_map.117.refs_4_
  51.6 0.7 %shard_map.115.refs_2_ = f32[256,512]{1,0:T(8,128)S(1)} custom-call(bf16[4096,512]{1,0:T(8,128)(2,1)S(1)} %copy-done, bf16[256,512]{1,0:T(8,128)(2,1)S(1)} %collective-permute-done.13.refs_0_, bf16[256,512]{1,0:T(8,128)(2,1)S(1)} %collective-permute-done.14.refs_1_, bf16[128,512]{1,0:T(8,128)(2,1)S(1)} %collective-permute-done.4.refs_2_, ...), custom_call_target="tpu_custom_call" | custom-call | tf_op jit(solution)/shard_map/pallas_call | solution.py:318
  52.4 0.3 shard_map.116.refs_3_
  52.7 0.0 collective-permute-done.20.refs_3_
  52.7 0.0 collective-permute-done.18.refs_1_
  52.7 0.7 %shard_map.118.refs_1_ = f32[256,512]{1,0:T(8,128)S(1)} custom-call(bf16[4096,512]{1,0:T(8,128)(2,1)S(1)} %copy-done, bf16[256,512]{1,0:T(8,128)(2,1)S(1)} %collective-permute-done.10.refs_0_, bf16[256,512]{1,0:T(8,128)(2,1)S(1)} %collective-permute-done.18.refs_1_, bf16[256,512]{1,0:T(8,128)(2,1)S(1)} %collective-permute-done.19.refs_2_, ...), custom_call_target="tpu_custom_call" | custom-call | tf_op jit(solution)/shard_map/pallas_call | solution.py:318
  53.4 0.3 shard_map.119.refs_4_
  53.7 0.0 collective-permute-done.6.refs_0_
  53.7 0.0 collective-permute-done.9.refs_1_
  53.7 0.0 collective-permute-done.12.refs_2_
  53.8 1.2 %store.1 = bf16[512,512]{1,0:T(8,128)(2,1)} custom-call(bf16[4096,512]{1,0:T(8,128)(2,1)S(1)} %copy-done, bf16[128,512]{1,0:T(8,128)(2,1)S(1)} %collective-permute-done.6.refs_0_, bf16[128,512]{1,0:T(8,128)(2,1)S(1)} %collective-permute-done.9.refs_1_, bf16[256,512]{1,0:T(8,128)(2,1)S(1)} %collective-permute-done.12.refs_2_, ...), custom_call_target="tpu_custom_call" | custom-call | tf_op jit(solution)/shard_map/store/pallas_call | solution.py:344
Async XLA Ops:
  3.4 10.0 %copy-start.1 = (bf16[4096,512]{1,0:T(8,128)(2,1)S(1)}, bf16[4096,512]{1,0:T(8,128)(2,1)}, u32[]{:S(2)}) copy-start(bf16[4096,512]{1,0:T(8,128)(2,1)} %weight.10) | copy-start | bytes 12582916
  4.8 4.4 %collective-permute-start = (bf16[256,256]{1,0:T(8,128)(2,1)S(1)}, bf16[256,256]{1,0:T(8,128)(2,1)S(1)}, u32[]{:S(2)}, u32[]{:S(2)}) collective-permute-start(bf16[256,256]{1,0:T(8,128)(2,1)S(1)} %get-tuple-element.27.refs_4_.refs_1_), channel_id=1, source_target_pairs={{0,8},{1,9},{2,10},{3,11},{4,12},{5,13},{6,14},{7,15},{8,16},{9,17... | collective-permute-start | bytes 393224 | tf_op jit(solution)/shard_map/ppermute | solution.py:380
  6.2 5.9 %collective-permute-start.2 = (bf16[256,256]{1,0:T(8,128)(2,1)S(1)}, bf16[256,256]{1,0:T(8,128)(2,1)S(1)}, u32[]{:S(2)}, u32[]{:S(2)}) collective-permute-start(bf16[256,256]{1,0:T(8,128)(2,1)S(1)} %get-tuple-element.28.refs_2_), channel_id=1, source_target_pairs={{0,8},{1,9},{2,10},{3,11},{4,12},{5,13},{6,14},{7,15},{8,16},{9,17... | collective-permute-start | bytes 393224 | tf_op jit(solution)/shard_map/ppermute | solution.py:380
  9.3 5.9 %collective-permute-start.1 = (bf16[256,256]{1,0:T(8,128)(2,1)S(1)}, bf16[256,256]{1,0:T(8,128)(2,1)S(1)}, u32[]{:S(2)}, u32[]{:S(2)}) collective-permute-start(bf16[256,256]{1,0:T(8,128)(2,1)S(1)} %collective-permute-done.refs_2_.refs_1_), channel_id=1, source_target_pairs={{8,16},{9,17},{10,18},{11,19},{12,20},{13,21},{14,22},{15,23},{16,... | collective-permute-start | bytes 393224 | tf_op jit(solution)/shard_map/ppermute | solution.py:380
  12.1 6.1 %collective-permute-start.3 = (bf16[256,256]{1,0:T(8,128)(2,1)S(1)}, bf16[256,256]{1,0:T(8,128)(2,1)S(1)}, u32[]{:S(2)}, u32[]{:S(2)}) collective-permute-start(bf16[256,256]{1,0:T(8,128)(2,1)S(1)} %collective-permute-done.2.refs_3_.refs_0_), channel_id=1, source_target_pairs={{8,16},{9,17},{10,18},{11,19},{12,20},{13,21},{14,22},{15,23},{16,... | collective-permute-start | bytes 393224 | tf_op jit(solution)/shard_map/ppermute | solution.py:380
  20.3 6.7 %collective-permute-start.4 = (bf16[128,512]{1,0:T(8,128)(2,1)S(1)}, bf16[128,512]{1,0:T(8,128)(2,1)S(1)}, u32[]{:S(2)}, u32[]{:S(2)}) collective-permute-start(bf16[128,512]{1,0:T(8,128)(2,1)S(1)} %get-tuple-element.29), channel_id=1, source_target_pairs={{0,4},{1,5},{2,6},{3,7},{4,0},{5,1},{6,2},{7,3},{8,12},{9,13},{10,... | collective-permute-start | bytes 393224 | tf_op jit(solution)/shard_map/ppermute | solution.py:385
  21.5 8.6 %collective-permute-start.7 = (bf16[128,512]{1,0:T(8,128)(2,1)S(1)}, bf16[128,512]{1,0:T(8,128)(2,1)S(1)}, u32[]{:S(2)}, u32[]{:S(2)}) collective-permute-start(bf16[128,512]{1,0:T(8,128)(2,1)S(1)} %get-tuple-element.30), channel_id=1, source_target_pairs={{0,4},{1,5},{2,6},{3,7},{4,0},{5,1},{6,2},{7,3},{8,12},{9,13},{10,... | collective-permute-start | bytes 393224 | tf_op jit(solution)/shard_map/ppermute | solution.py:385
  21.8 29.0 %copy-start = (bf16[4096,512]{1,0:T(8,128)(2,1)S(1)}, bf16[4096,512]{1,0:T(8,128)(2,1)}, u32[]{:S(2)}) copy-start(bf16[4096,512]{1,0:T(8,128)(2,1)} %weight.17) | copy-start | bytes 12582916
  25.6 15.9 %collective-permute-start.10 = (bf16[256,512]{1,0:T(8,128)(2,1)S(1)}, bf16[256,512]{1,0:T(8,128)(2,1)S(1)}, u32[]{:S(2)}, u32[]{:S(2)}) collective-permute-start(bf16[256,512]{1,0:T(8,128)(2,1)S(1)} %shard_map.113.refs_0_), channel_id=1, source_target_pairs={{0,2},{1,3},{2,0},{3,1},{4,6},{5,7},{6,4},{7,5},{8,10},{9,11},{10,... | collective-permute-start | bytes 786440 | tf_op jit(solution)/shard_map/ppermute | solution.py:385
  26.9 4.7 %collective-permute-start.15 = (bf16[128,512]{1,0:T(8,128)(2,1)S(1)}, bf16[128,512]{1,0:T(8,128)(2,1)S(1)}, u32[]{:S(2)}, u32[]{:S(2)}) collective-permute-start(bf16[128,512]{1,0:T(8,128)(2,1)S(1)} %collective-permute-done.4.refs_2_), channel_id=1, source_target_pairs={{0,1},{1,0},{2,3},{3,2},{4,5},{5,4},{6,7},{7,6},{8,9},{9,8},{10,11... | collective-permute-start | bytes 393224 | tf_op jit(solution)/shard_map/ppermute | solution.py:385
  29.9 5.5 %collective-permute-start.5 = (bf16[128,512]{1,0:T(8,128)(2,1)S(1)}, bf16[128,512]{1,0:T(8,128)(2,1)S(1)}, u32[]{:S(2)}, u32[]{:S(2)}) collective-permute-start(bf16[128,512]{1,0:T(8,128)(2,1)S(1)} %collective-permute-done.4.refs_2_), channel_id=1, source_target_pairs={{0,2},{1,3},{2,0},{3,1},{4,6},{5,7},{6,4},{7,5},{8,10},{9,11},{10,... | collective-permute-start | bytes 393224 | tf_op jit(solution)/shard_map/ppermute | solution.py:385
  30.1 9.2 %collective-permute-start.16 = (bf16[128,512]{1,0:T(8,128)(2,1)S(1)}, bf16[128,512]{1,0:T(8,128)(2,1)S(1)}, u32[]{:S(2)}, u32[]{:S(2)}) collective-permute-start(bf16[128,512]{1,0:T(8,128)(2,1)S(1)} %collective-permute-done.7.refs_3_), channel_id=1, source_target_pairs={{0,1},{1,0},{2,3},{3,2},{4,5},{5,4},{6,7},{7,6},{8,9},{9,8},{10,11... | collective-permute-start | bytes 393224 | tf_op jit(solution)/shard_map/ppermute | solution.py:385
  30.4 15.6 %collective-permute-start.13 = (bf16[256,512]{1,0:T(8,128)(2,1)S(1)}, bf16[256,512]{1,0:T(8,128)(2,1)S(1)}, u32[]{:S(2)}, u32[]{:S(2)}) collective-permute-start(bf16[256,512]{1,0:T(8,128)(2,1)S(1)} %get-tuple-element.34.refs_0_), channel_id=1, source_target_pairs={{0,2},{1,3},{2,0},{3,1},{4,6},{5,7},{6,4},{7,5},{8,10},{9,11},{10,... | collective-permute-start | bytes 786440 | tf_op jit(solution)/shard_map/ppermute | solution.py:385
  31.6 14.4 %collective-permute-start.19 = (bf16[256,512]{1,0:T(8,128)(2,1)S(1)}, bf16[256,512]{1,0:T(8,128)(2,1)S(1)}, u32[]{:S(2)}, u32[]{:S(2)}) collective-permute-start(bf16[256,512]{1,0:T(8,128)(2,1)S(1)} %shard_map.113.refs_0_), channel_id=1, source_target_pairs={{0,4},{1,5},{2,6},{3,7},{4,0},{5,1},{6,2},{7,3},{8,12},{9,13},{10,... | collective-permute-start | bytes 786440 | tf_op jit(solution)/shard_map/ppermute | solution.py:385
  35.4 11.1 %collective-permute-start.17 = (bf16[256,512]{1,0:T(8,128)(2,1)S(1)}, bf16[256,512]{1,0:T(8,128)(2,1)S(1)}, u32[]{:S(2)}, u32[]{:S(2)}) collective-permute-start(bf16[256,512]{1,0:T(8,128)(2,1)S(1)} %get-tuple-element.34.refs_0_), channel_id=1, source_target_pairs={{0,1},{1,0},{2,3},{3,2},{4,5},{5,4},{6,7},{7,6},{8,9},{9,8},{10,11... | collective-permute-start | bytes 786440 | tf_op jit(solution)/shard_map/ppermute | solution.py:385
  39.3 6.1 %collective-permute-start.8 = (bf16[128,512]{1,0:T(8,128)(2,1)S(1)}, bf16[128,512]{1,0:T(8,128)(2,1)S(1)}, u32[]{:S(2)}, u32[]{:S(2)}) collective-permute-start(bf16[128,512]{1,0:T(8,128)(2,1)S(1)} %collective-permute-done.7.refs_3_), channel_id=1, source_target_pairs={{0,2},{1,3},{2,0},{3,1},{4,6},{5,7},{6,4},{7,5},{8,10},{9,11},{10,... | collective-permute-start | bytes 393224 | tf_op jit(solution)/shard_map/ppermute | solution.py:385
  41.5 7.6 %collective-permute-start.11 = (bf16[256,512]{1,0:T(8,128)(2,1)S(1)}, bf16[256,512]{1,0:T(8,128)(2,1)S(1)}, u32[]{:S(2)}, u32[]{:S(2)}) collective-permute-start(bf16[256,512]{1,0:T(8,128)(2,1)S(1)} %collective-permute-done.10.refs_0_), channel_id=1, source_target_pairs={{0,4},{1,5},{2,6},{3,7},{4,0},{5,1},{6,2},{7,3},{8,12},{9,13},{10,... | collective-permute-start | bytes 786440 | tf_op jit(solution)/shard_map/ppermute | solution.py:385
  45.4 4.8 %collective-permute-start.21 = (bf16[256,512]{1,0:T(8,128)(2,1)S(1)}, bf16[256,512]{1,0:T(8,128)(2,1)S(1)}, u32[]{:S(2)}, u32[]{:S(2)}) collective-permute-start(bf16[256,512]{1,0:T(8,128)(2,1)S(1)} %shard_map.113.refs_0_), channel_id=1, source_target_pairs={{0,1},{1,0},{2,3},{3,2},{4,5},{5,4},{6,7},{7,6},{8,9},{9,8},{10,11... | collective-permute-start | bytes 786440 | tf_op jit(solution)/shard_map/ppermute | solution.py:385
  46.0 4.3 %collective-permute-start.14 = (bf16[256,512]{1,0:T(8,128)(2,1)S(1)}, bf16[256,512]{1,0:T(8,128)(2,1)S(1)}, u32[]{:S(2)}, u32[]{:S(2)}) collective-permute-start(bf16[256,512]{1,0:T(8,128)(2,1)S(1)} %collective-permute-done.13.refs_0_), channel_id=1, source_target_pairs={{0,1},{1,0},{2,3},{3,2},{4,5},{5,4},{6,7},{7,6},{8,9},{9,8},{10,11... | collective-permute-start | bytes 786440 | tf_op jit(solution)/shard_map/ppermute | solution.py:385
  46.0 6.7 %collective-permute-start.20 = (bf16[256,512]{1,0:T(8,128)(2,1)S(1)}, bf16[256,512]{1,0:T(8,128)(2,1)S(1)}, u32[]{:S(2)}, u32[]{:S(2)}) collective-permute-start(bf16[256,512]{1,0:T(8,128)(2,1)S(1)} %collective-permute-done.19.refs_2_), channel_id=1, source_target_pairs={{0,1},{1,0},{2,3},{3,2},{4,5},{5,4},{6,7},{7,6},{8,9},{9,8},{10,11... | collective-permute-start | bytes 786440 | tf_op jit(solution)/shard_map/ppermute | solution.py:385
  46.5 6.2 %collective-permute-start.18 = (bf16[256,512]{1,0:T(8,128)(2,1)S(1)}, bf16[256,512]{1,0:T(8,128)(2,1)S(1)}, u32[]{:S(2)}, u32[]{:S(2)}) collective-permute-start(bf16[256,512]{1,0:T(8,128)(2,1)S(1)} %collective-permute-done.10.refs_0_), channel_id=1, source_target_pairs={{0,1},{1,0},{2,3},{3,2},{4,5},{5,4},{6,7},{7,6},{8,9},{9,8},{10,11... | collective-permute-start | bytes 786440 | tf_op jit(solution)/shard_map/ppermute | solution.py:385
  49.1 4.7 %collective-permute-start.12 = (bf16[256,512]{1,0:T(8,128)(2,1)S(1)}, bf16[256,512]{1,0:T(8,128)(2,1)S(1)}, u32[]{:S(2)}, u32[]{:S(2)}) collective-permute-start(bf16[256,512]{1,0:T(8,128)(2,1)S(1)} %collective-permute-done.11.refs_0_), channel_id=1, source_target_pairs={{0,1},{1,0},{2,3},{3,2},{4,5},{5,4},{6,7},{7,6},{8,9},{9,8},{10,11... | collective-permute-start | bytes 786440 | tf_op jit(solution)/shard_map/ppermute | solution.py:385
  50.2 3.5 %collective-permute-start.6 = (bf16[128,512]{1,0:T(8,128)(2,1)S(1)}, bf16[128,512]{1,0:T(8,128)(2,1)S(1)}, u32[]{:S(2)}, u32[]{:S(2)}) collective-permute-start(bf16[128,512]{1,0:T(8,128)(2,1)S(1)} %collective-permute-done.5.refs_0_), channel_id=1, source_target_pairs={{0,1},{1,0},{2,3},{3,2},{4,5},{5,4},{6,7},{7,6},{8,9},{9,8},{10,11... | collective-permute-start | bytes 393224 | tf_op jit(solution)/shard_map/ppermute | solution.py:385
  50.2 3.5 %collective-permute-start.9 = (bf16[128,512]{1,0:T(8,128)(2,1)S(1)}, bf16[128,512]{1,0:T(8,128)(2,1)S(1)}, u32[]{:S(2)}, u32[]{:S(2)}) collective-permute-start(bf16[128,512]{1,0:T(8,128)(2,1)S(1)} %collective-permute-done.8.refs_1_), channel_id=1, source_target_pairs={{0,1},{1,0},{2,3},{3,2},{4,5},{5,4},{6,7},{7,6},{8,9},{9,8},{10,11... | collective-permute-start | bytes 393224 | tf_op jit(solution)/shard_map/ppermute | solution.py:385
where the time goes:
time: 55.2 us; the launch traced here: 55.1 us
  starting transfers between devices  24.1 us (44%)
  Pallas kernels  16.2 us (29%)
  waiting for transfers between devices  14.5 us (26%)
    ppermute x18, starting transfers between devices, swap(): return lax.ppermute(x, 'tp', [(i, i ^ bit) for i in range(tp_count)])  18.9 us
    ppermute x18, waiting for transfers between devices, swap(): return lax.ppermute(x, 'tp', [(i, i ^ bit) for i in range(tp_count)])  7.74 us
    ppermute x4, waiting for transfers between devices, shards(): lax.ppermute(halves[distance - 2], ('seq', 'tp'), onward(distance // 2))  6.72 us
    ppermute x4, starting transfers between devices, shards(): lax.ppermute(halves[distance - 2], ('seq', 'tp'), onward(distance // 2))  5.24 us
    pallas_call x3, Pallas kernels, attend(): pl.pallas_call(functools.partial(attend_kernel, part, back, tuple(places)...  4.5 us
    pallas_call x1, Pallas kernels, second_half(): pl.pallas_call(functools.partial(second_half_kernel, tile), out_shape=(sh...  3.4 us
    pallas_call x6, Pallas kernels, product(): pl.pallas_call(functools.partial(product_kernel, bits, counts), out_shape...  2.91 us
    pallas_call x2, Pallas kernels, query(): pl.pallas_call(functools.partial(query_kernel, part), out_shape=jax.Shape...  2.76 us
  transfers between devices with their start and end apart: 22, of which 7 were waited for; matrix products, arithmetic and copies ran while one was open for 0% of the time, Pallas kernels for 15%

commit v1 on v0

--- a/solution.py
+++ b/solution.py
@@ -287,9 +287,9 @@
 
 
 def added(bits, total, weight, pieces):
-    depth = pieces[0][0].shape[1]
     me = lax.axis_index("tp")
     for bit, piece in zip(bits, pieces):
+        depth = piece[0].shape[1]
         owner = jnp.bitwise_xor(me, bit)
         rows = pl.ds(pl.multiple_of(owner * depth, depth), depth)
         x = jnp.concatenate([a[...] for a in piece], axis=0) if len(piece) > 1 else piece[0][...]
@@ -331,7 +331,7 @@
     moves = []
     for part in (1, 0):
         rows = slice(part * half, (part + 1) * half)
-        rounded[rows, :] = added(bits[part], totals[part][...], weight, [pieces[part]]).astype(rounded.dtype)
+        rounded[rows, :] = added(bits[part], totals[part][...], weight, pieces[part : part + 1]).astype(rounded.dtype)
         moves.append(pltpu.make_async_copy(rounded.at[rows, :], out_ref.at[rows, :], sems.at[part]))
         moves[-1].start()
     for move in moves:
@@ -342,7 +342,7 @@
     xs = [a for piece in pieces for a in piece]
     half, width = totals[0].shape
     return pl.pallas_call(
-        functools.partial(store_kernel, [(bits,)] * 2, [len(piece) for piece in pieces]),
+        functools.partial(store_kernel, [(bits,), ()], [len(piece) for piece in pieces]),
         out_shape=pltpu.HBM((2 * half, width), jnp.bfloat16),
         in_specs=[VMEM] * (3 + len(xs)),
         out_specs=HBM,
@@ -405,10 +405,10 @@
     for part in (1, 0):
         pieces = lambda *bits: [(b, got[part][b]) for b in bits]
         acc = None
-        for bits in ((0, 1), (2, 3, 4, 5), (6,)):
+        for bits in ((0, 1), (2, 3, 4, 5), (6, 7) if part == 1 else (6,)):
             acc = product(out_weight, pieces(*bits), acc)
         totals[part] = acc
-    return store(out_weight, 7, [got[part][7] for part in (0, 1)], totals)
+    return store(out_weight, 7, [got[0][7]], totals)
 
 
 def solution(mesh):

time: 55.2 us -> 55.7 us (level)
  the two profiles are of different devices: /device:TPU:9 before, /device:TPU:0 now
where the time goes in v1:
time: 55.7 us; the launch traced here: 55.5 us
  waiting for transfers between devices  23 us (41%)
  Pallas kernels  16.2 us (29%)
  starting transfers between devices  16 us (29%)
    ppermute x18, waiting for transfers between devices, swap(): return lax.ppermute(x, 'tp', [(i, i ^ bit) for i in range(tp_count)])  15.4 us
    ppermute x18, starting transfers between devices, swap(): return lax.ppermute(x, 'tp', [(i, i ^ bit) for i in range(tp_count)])  11.3 us
    ppermute x4, waiting for transfers between devices, shards(): lax.ppermute(halves[distance - 2], ('seq', 'tp'), onward(distance // 2))  7.61 us
    ppermute x4, starting transfers between devices, shards(): lax.ppermute(halves[distance - 2], ('seq', 'tp'), onward(distance // 2))  4.69 us
    pallas_call x3, Pallas kernels, attend(): pl.pallas_call(functools.partial(attend_kernel, part, back, tuple(places)...  4.5 us
    pallas_call x1, Pallas kernels, second_half(): pl.pallas_call(functools.partial(second_half_kernel, tile), out_shape=(sh...  3.4 us
    pallas_call x6, Pallas kernels, product(): pl.pallas_call(functools.partial(product_kernel, bits, counts), out_shape...  3.05 us
    pallas_call x2, Pallas kernels, query(): pl.pallas_call(functools.partial(query_kernel, part), out_shape=jax.Shape...  2.76 us
  transfers between devices with their start and end apart: 22, of which 7 were waited for; matrix products, arithmetic and copies ran while one was open for 0% of the time, Pallas kernels for 15%

profile of v1, /device:TPU:0, one launch (start us, length us, event | category | flops | bytes accessed | tf_op | source)
XLA Modules:
  0.0 55.5 jit_solution(8304403403284420833)
XLA Ops:
  0.0 3.4 %second_half.1 = (bf16[256,256]{1,0:T(8,128)(2,1)S(1)}, bf16[256,4096]{1,0:T(8,128)(2,1)S(1)}, bf16[4096,256]{1,0:T(8,128)(2,1)S(1)}, bf16[256,4096]{1,0:T(8,128...) custom-call(bf16[512,4096]{1,0:T(8,128)(2,1)} %tokens.1, ...), custom_call_target="tpu_custom_call" | custom-call | tf_op jit(solution)/shard_map/second_half/pallas_call | solution.py:122
  3.4 0.0 copy-start.1
  3.4 1.4 %first_half.1 = (bf16[256,256]{1,0:T(8,128)(2,1)S(1)}, bf16[256,4096]{1,0:T(8,128)(2,1)S(1)}) custom-call(bf16[256,4096]{1,0:T(8,128)(2,1)S(1)} %get-tuple-element.21.tokens, f32[1,4096]{1,0:T(1,128)S(1)} %get-tuple-element.22.gain, bf16[4096,256]{1,0:T(8,128)(2,1)S(1)} %get-tuple-element.23.weight, f32[512,128]{1,0:T(8,128)S(1)} %get-tuple-element.24.cosine, ...), custom_call_target="tpu_custom_call" | custom-call | tf_op jit(solution)/shard_map/first_half/pallas_call | solution.py:154
  4.8 3.1 %collective-permute-start = (bf16[256,256]{1,0:T(8,128)(2,1)S(1)}, bf16[256,256]{1,0:T(8,128)(2,1)S(1)}, u32[]{:S(2)}, u32[]{:S(2)}) collective-permute-start(bf16[256,256]{1,0:T(8,128)(2,1)S(1)} %get-tuple-element.27.refs_4_.refs_1_), channel_id=1, source_target_pairs={{0,8},{1,9},{2,10},{3,11},{4,12},{5,13},{6,14},{7,15},{8,16},{9,17... | collective-permute-start | bytes 393224 | tf_op jit(solution)/shard_map/ppermute | solution.py:380
  7.9 1.6 %collective-permute-start.2 = (bf16[256,256]{1,0:T(8,128)(2,1)S(1)}, bf16[256,256]{1,0:T(8,128)(2,1)S(1)}, u32[]{:S(2)}, u32[]{:S(2)}) collective-permute-start(bf16[256,256]{1,0:T(8,128)(2,1)S(1)} %get-tuple-element.28.refs_2_), channel_id=1, source_target_pairs={{0,8},{1,9},{2,10},{3,11},{4,12},{5,13},{6,14},{7,15},{8,16},{9,17... | collective-permute-start | bytes 393224 | tf_op jit(solution)/shard_map/ppermute | solution.py:380
  9.5 4.8 %collective-permute-done.refs_2_.refs_1_ = bf16[256,256]{1,0:T(8,128)(2,1)S(1)} collective-permute-done((bf16[256,256]{1,0:T(8,128)(2,1)S(1)}, bf16[256,256]{1,0:T(8,128)(2,1)S(1)}, u32[]{:S(2)}, u32[]{:S(2)}) %collective-permute-start) | collective-permute-done | bytes 131104 | tf_op jit(solution)/shard_map/ppermute | solution.py:380
  14.3 0.0 collective-permute-start.1
  14.3 2.8 %collective-permute-done.2.refs_3_.refs_0_ = bf16[256,256]{1,0:T(8,128)(2,1)S(1)} collective-permute-done((bf16[256,256]{1,0:T(8,128)(2,1)S(1)}, bf16[256,256]{1,0:T(8,128)(2,1)S(1)}, u32[]{:S(2)}, u32[]{:S(2)}) %collective-permute-start.2) | collective-permute-done | bytes 131104 | tf_op jit(solution)/shard_map/ppermute | solution.py:380
  17.1 0.0 collective-permute-start.3
  17.1 0.0 copy-done.1
  17.1 1.4 %shard_map.109.q_ref = bf16[256,512]{1,0:T(8,128)(2,1)S(1)} custom-call(bf16[256,4096]{1,0:T(8,128)(2,1)S(1)} %get-tuple-element.26.normed, bf16[4096,512]{1,0:T(8,128)(2,1)S(1)} %copy-done.1, f32[512,128]{1,0:T(8,128)S(1)} %get-tuple-element.24.cosine, f32[512,128]{1,0:T(8,128)S(1)} %get-tuple-element.25.sine), custom_call_target="tpu_custom_call" | custom-call | tf_op jit(solution)/shard_map/pallas_call | solution.py:175
  18.5 0.0 collective-permute-done.1.refs_0_
  18.5 0.0 collective-permute-done.3.refs_1_.refs_0_
  18.5 2.1 %shard_map.110 = (bf16[256,512]{1,0:T(8,128)(2,1)S(1)}, bf16[128,512]{1,0:T(8,128)(2,1)S(1)}, bf16[128,512]{1,0:T(8,128)(2,1)S(1)}) custom-call(s32[2,128]{1,0:T(2,128)S(1)} %get-tuple-element.20.limits, bf16[256,512]{1,0:T(8,128)(2,1)S(1)} %shard_map.109.q_ref, bf16[256,256]{1,0:T(8,128)(2,1)S(1)} %collective-permute-done.1.refs_0_, ...), custom_call_target="tpu_custom_call" | custom-call | tf_op jit(solution)/shard_map/pallas_call | solution.py:279
  20.6 1.8 %collective-permute-start.4 = (bf16[128,512]{1,0:T(8,128)(2,1)S(1)}, bf16[128,512]{1,0:T(8,128)(2,1)S(1)}, u32[]{:S(2)}, u32[]{:S(2)}) collective-permute-start(bf16[128,512]{1,0:T(8,128)(2,1)S(1)} %get-tuple-element.29), channel_id=1, source_target_pairs={{0,4},{1,5},{2,6},{3,7},{4,0},{5,1},{6,2},{7,3},{8,12},{9,13},{10,... | collective-permute-start | bytes 393224 | tf_op jit(solution)/shard_map/ppermute | solution.py:385
  22.4 0.0 copy-start
  22.4 1.4 %shard_map.114.q_ref = bf16[256,512]{1,0:T(8,128)(2,1)S(1)} custom-call(bf16[256,4096]{1,0:T(8,128)(2,1)S(1)} %get-tuple-element.32.normed, bf16[4096,512]{1,0:T(8,128)(2,1)S(1)} %copy-done.1, f32[512,128]{1,0:T(8,128)S(1)} %get-tuple-element.24.cosine, f32[512,128]{1,0:T(8,128)S(1)} %get-tuple-element.25.sine), custom_call_target="tpu_custom_call" | custom-call | tf_op jit(solution)/shard_map/pallas_call | solution.py:175
  23.8 1.4 %shard_map.115 = (f32[256,1024]{1,0:T(8,128)S(1)}, f32[256,512]{1,0:T(8,128)S(1)}) custom-call(s32[2,128]{1,0:T(2,128)S(1)} %get-tuple-element.20.limits, bf16[256,512]{1,0:T(8,128)(2,1)S(1)} %shard_map.114.q_ref, bf16[256,256]{1,0:T(8,128)(2,1)S(1)} %collective-permute-done.2.refs_3_.refs_0_, bf16[256,256]{1,0:T(8,128)(2,1)S(1)} %get-tuple-element.27.refs_4_.refs_1_, ...), custom_call_target="tpu_custom_call" | custom-call | tf_op jit(solution)/shard_map/pallas_call | solution.py:279
  25.2 0.4 collective-permute-start.7
  25.5 1.1 %shard_map.116.refs_0_ = bf16[256,512]{1,0:T(8,128)(2,1)S(1)} custom-call(s32[2,128]{1,0:T(2,128)S(1)} %get-tuple-element.20.limits, bf16[256,512]{1,0:T(8,128)(2,1)S(1)} %shard_map.114.q_ref, bf16[256,256]{1,0:T(8,128)(2,1)S(1)} %collective-permute-done.3.refs_1_.refs_0_, bf16[256,256]{1,0:T(8,128)(2,1)S(1)} %collective-permute-done.refs_2_.refs_1_, ...), custom_call_target="tpu_custom_call" | custom-call | tf_op jit(solution)/shard_map/pallas_call | solution.py:279
  26.6 1.8 %collective-permute-start.15 = (bf16[256,512]{1,0:T(8,128)(2,1)S(1)}, bf16[256,512]{1,0:T(8,128)(2,1)S(1)}, u32[]{:S(2)}, u32[]{:S(2)}) collective-permute-start(bf16[256,512]{1,0:T(8,128)(2,1)S(1)} %shard_map.116.refs_0_), channel_id=1, source_target_pairs={{0,2},{1,3},{2,0},{3,1},{4,6},{5,7},{6,4},{7,5},{8,10},{9,11},{10,... | collective-permute-start | bytes 786440 | tf_op jit(solution)/shard_map/ppermute | solution.py:385
  28.4 0.0 collective-permute-done.4.refs_2_
  28.4 0.0 collective-permute-start.12
  28.4 0.3 collective-permute-start.5
  28.7 2.2 %collective-permute-done.7.refs_3_ = bf16[128,512]{1,0:T(8,128)(2,1)S(1)} collective-permute-done((bf16[128,512]{1,0:T(8,128)(2,1)S(1)}, bf16[128,512]{1,0:T(8,128)(2,1)S(1)}, u32[]{:S(2)}, u32[]{:S(2)}) %collective-permute-start.7) | collective-permute-done | bytes 131104 | tf_op jit(solution)/shard_map/ppermute | solution.py:385
  30.9 0.0 collective-permute-start.13
  30.9 1.5 %collective-permute-start.10 = (bf16[256,512]{1,0:T(8,128)(2,1)S(1)}, bf16[256,512]{1,0:T(8,128)(2,1)S(1)}, u32[]{:S(2)}, u32[]{:S(2)}) collective-permute-start(bf16[256,512]{1,0:T(8,128)(2,1)S(1)} %get-tuple-element.31.refs_0_), channel_id=1, source_target_pairs={{0,2},{1,3},{2,0},{3,1},{4,6},{5,7},{6,4},{7,5},{8,10},{9,11},{10,... | collective-permute-start | bytes 786440 | tf_op jit(solution)/shard_map/ppermute | solution.py:385
  32.4 0.0 collective-permute-done.12.refs_4_
  32.4 0.2 collective-permute-start.14
  32.6 6.1 %collective-permute-done.5.refs_0_ = bf16[128,512]{1,0:T(8,128)(2,1)S(1)} collective-permute-done((bf16[128,512]{1,0:T(8,128)(2,1)S(1)}, bf16[128,512]{1,0:T(8,128)(2,1)S(1)}, u32[]{:S(2)}, u32[]{:S(2)}) %collective-permute-start.5) | collective-permute-done | bytes 131104 | tf_op jit(solution)/shard_map/ppermute | solution.py:385
  38.7 1.7 %collective-permute-start.19 = (bf16[256,512]{1,0:T(8,128)(2,1)S(1)}, bf16[256,512]{1,0:T(8,128)(2,1)S(1)}, u32[]{:S(2)}, u32[]{:S(2)}) collective-permute-start(bf16[256,512]{1,0:T(8,128)(2,1)S(1)} %shard_map.116.refs_0_), channel_id=1, source_target_pairs={{0,4},{1,5},{2,6},{3,7},{4,0},{5,1},{6,2},{7,3},{8,12},{9,13},{10,... | collective-permute-start | bytes 786440 | tf_op jit(solution)/shard_map/ppermute | solution.py:385
  40.4 0.0 collective-permute-done.13.refs_5_
  40.4 1.5 %collective-permute-start.8 = (bf16[128,512]{1,0:T(8,128)(2,1)S(1)}, bf16[128,512]{1,0:T(8,128)(2,1)S(1)}, u32[]{:S(2)}, u32[]{:S(2)}) collective-permute-start(bf16[128,512]{1,0:T(8,128)(2,1)S(1)} %collective-permute-done.7.refs_3_), channel_id=1, source_target_pairs={{0,2},{1,3},{2,0},{3,1},{4,6},{5,7},{6,4},{7,5},{8,10},{9,11},{10,... | collective-permute-start | bytes 393224 | tf_op jit(solution)/shard_map/ppermute | solution.py:385
  41.9 0.0 collective-permute-done.15.refs_0_
  41.9 0.5 collective-permute-start.16
  42.4 3.7 %collective-permute-done.8.refs_1_ = bf16[128,512]{1,0:T(8,128)(2,1)S(1)} collective-permute-done((bf16[128,512]{1,0:T(8,128)(2,1)S(1)}, bf16[128,512]{1,0:T(8,128)(2,1)S(1)}, u32[]{:S(2)}, u32[]{:S(2)}) %collective-permute-start.8) | collective-permute-done | bytes 131104 | tf_op jit(solution)/shard_map/ppermute | solution.py:385
  46.1 0.0 collective-permute-start.21
  46.1 0.0 collective-permute-done.10.refs_0_
  46.1 0.5 collective-permute-start.11
  46.6 1.2 %collective-permute-done.19.refs_2_ = bf16[256,512]{1,0:T(8,128)(2,1)S(1)} collective-permute-done((bf16[256,512]{1,0:T(8,128)(2,1)S(1)}, bf16[256,512]{1,0:T(8,128)(2,1)S(1)}, u32[]{:S(2)}, u32[]{:S(2)}) %collective-permute-start.19) | collective-permute-done | bytes 262176 | tf_op jit(solution)/shard_map/ppermute | solution.py:385
  47.8 0.0 collective-permute-start.20
  47.8 0.0 collective-permute-done.14.refs_1_
  47.8 0.5 collective-permute-start.18
  48.3 2.3 %collective-permute-done.16.refs_0_ = bf16[256,512]{1,0:T(8,128)(2,1)S(1)} collective-permute-done((bf16[256,512]{1,0:T(8,128)(2,1)S(1)}, bf16[256,512]{1,0:T(8,128)(2,1)S(1)}, u32[]{:S(2)}, u32[]{:S(2)}) %collective-permute-start.16) | collective-permute-done | bytes 262176 | tf_op jit(solution)/shard_map/ppermute | solution.py:385
  50.6 0.0 collective-permute-start.17
  50.6 0.0 collective-permute-done.21.refs_1_
  50.6 0.5 collective-permute-start.6
  51.1 0.0 collective-permute-done.11.refs_1_
  51.1 0.1 collective-permute-start.9
  51.2 0.0 copy-done
  51.2 0.4 shard_map.111.refs_6_
  51.6 0.4 shard_map.117.refs_4_
  52.1 0.7 %shard_map.112.refs_2_ = f32[256,512]{1,0:T(8,128)S(1)} custom-call(bf16[4096,512]{1,0:T(8,128)(2,1)S(1)} %copy-done, bf16[256,512]{1,0:T(8,128)(2,1)S(1)} %collective-permute-done.10.refs_0_, bf16[256,512]{1,0:T(8,128)(2,1)S(1)} %collective-permute-done.11.refs_1_, bf16[128,512]{1,0:T(8,128)(2,1)S(1)} %collective-permute-done.4.refs_2_, ...), custom_call_target="tpu_custom_call" | custom-call | tf_op jit(solution)/shard_map/pallas_call | solution.py:318
  52.8 0.3 shard_map.113.refs_2_
  53.1 0.0 collective-permute-done.20.refs_3_
  53.1 0.0 collective-permute-done.18.refs_1_
  53.1 0.7 %shard_map.118.refs_2_ = f32[256,512]{1,0:T(8,128)S(1)} custom-call(bf16[4096,512]{1,0:T(8,128)(2,1)S(1)} %copy-done, bf16[256,512]{1,0:T(8,128)(2,1)S(1)} %collective-permute-done.15.refs_0_, bf16[256,512]{1,0:T(8,128)(2,1)S(1)} %collective-permute-done.18.refs_1_, bf16[256,512]{1,0:T(8,128)(2,1)S(1)} %collective-permute-done.19.refs_2_, ...), custom_call_target="tpu_custom_call" | custom-call | tf_op jit(solution)/shard_map/pallas_call | solution.py:318
  53.8 0.0 collective-permute-done.17.refs_1_
  53.9 0.4 shard_map.119.refs_3_
  54.3 0.0 collective-permute-done.6.refs_0_
  54.3 0.0 collective-permute-done.9.refs_1_
  54.3 1.0 %store.1 = bf16[512,512]{1,0:T(8,128)(2,1)} custom-call(bf16[4096,512]{1,0:T(8,128)(2,1)S(1)} %copy-done, bf16[128,512]{1,0:T(8,128)(2,1)S(1)} %collective-permute-done.6.refs_0_, bf16[128,512]{1,0:T(8,128)(2,1)S(1)} %collective-permute-done.9.refs_1_, f32[256,512]{1,0:T(8,128)S(1)} %shard_map.113.refs_2_, f32[256,512]{1,0:T(8,128)S(1)} %shard_map.119.refs_3_), custom_call_target="tpu_custom_call" | custom-call | tf_op jit(solution)/shard_map/store/pallas_call | solution.py:344
Async XLA Ops:
  3.4 13.7 %copy-start.1 = (bf16[4096,512]{1,0:T(8,128)(2,1)S(1)}, bf16[4096,512]{1,0:T(8,128)(2,1)}, u32[]{:S(2)}) copy-start(bf16[4096,512]{1,0:T(8,128)(2,1)} %weight.13) | copy-start | bytes 12582916
  4.8 9.5 %collective-permute-start = (bf16[256,256]{1,0:T(8,128)(2,1)S(1)}, bf16[256,256]{1,0:T(8,128)(2,1)S(1)}, u32[]{:S(2)}, u32[]{:S(2)}) collective-permute-start(bf16[256,256]{1,0:T(8,128)(2,1)S(1)} %get-tuple-element.27.refs_4_.refs_1_), channel_id=1, source_target_pairs={{0,8},{1,9},{2,10},{3,11},{4,12},{5,13},{6,14},{7,15},{8,16},{9,17... | collective-permute-start | bytes 393224 | tf_op jit(solution)/shard_map/ppermute | solution.py:380
  7.9 9.2 %collective-permute-start.2 = (bf16[256,256]{1,0:T(8,128)(2,1)S(1)}, bf16[256,256]{1,0:T(8,128)(2,1)S(1)}, u32[]{:S(2)}, u32[]{:S(2)}) collective-permute-start(bf16[256,256]{1,0:T(8,128)(2,1)S(1)} %get-tuple-element.28.refs_2_), channel_id=1, source_target_pairs={{0,8},{1,9},{2,10},{3,11},{4,12},{5,13},{6,14},{7,15},{8,16},{9,17... | collective-permute-start | bytes 393224 | tf_op jit(solution)/shard_map/ppermute | solution.py:380
  14.3 4.2 %collective-permute-start.1 = (bf16[256,256]{1,0:T(8,128)(2,1)S(1)}, bf16[256,256]{1,0:T(8,128)(2,1)S(1)}, u32[]{:S(2)}, u32[]{:S(2)}) collective-permute-start(bf16[256,256]{1,0:T(8,128)(2,1)S(1)} %collective-permute-done.refs_2_.refs_1_), channel_id=1, source_target_pairs={{8,16},{9,17},{10,18},{11,19},{12,20},{13,21},{14,22},{15,23},{16,... | collective-permute-start | bytes 393224 | tf_op jit(solution)/shard_map/ppermute | solution.py:380
  17.1 1.4 %collective-permute-start.3 = (bf16[256,256]{1,0:T(8,128)(2,1)S(1)}, bf16[256,256]{1,0:T(8,128)(2,1)S(1)}, u32[]{:S(2)}, u32[]{:S(2)}) collective-permute-start(bf16[256,256]{1,0:T(8,128)(2,1)S(1)} %collective-permute-done.2.refs_3_.refs_0_), channel_id=1, source_target_pairs={{8,16},{9,17},{10,18},{11,19},{12,20},{13,21},{14,22},{15,23},{16,... | collective-permute-start | bytes 393224 | tf_op jit(solution)/shard_map/ppermute | solution.py:380
  20.6 7.8 %collective-permute-start.4 = (bf16[128,512]{1,0:T(8,128)(2,1)S(1)}, bf16[128,512]{1,0:T(8,128)(2,1)S(1)}, u32[]{:S(2)}, u32[]{:S(2)}) collective-permute-start(bf16[128,512]{1,0:T(8,128)(2,1)S(1)} %get-tuple-element.29), channel_id=1, source_target_pairs={{0,4},{1,5},{2,6},{3,7},{4,0},{5,1},{6,2},{7,3},{8,12},{9,13},{10,... | collective-permute-start | bytes 393224 | tf_op jit(solution)/shard_map/ppermute | solution.py:385
  22.4 28.8 %copy-start = (bf16[4096,512]{1,0:T(8,128)(2,1)S(1)}, bf16[4096,512]{1,0:T(8,128)(2,1)}, u32[]{:S(2)}) copy-start(bf16[4096,512]{1,0:T(8,128)(2,1)} %weight.17) | copy-start | bytes 12582916
  25.2 5.7 %collective-permute-start.7 = (bf16[128,512]{1,0:T(8,128)(2,1)S(1)}, bf16[128,512]{1,0:T(8,128)(2,1)S(1)}, u32[]{:S(2)}, u32[]{:S(2)}) collective-permute-start(bf16[128,512]{1,0:T(8,128)(2,1)S(1)} %get-tuple-element.30), channel_id=1, source_target_pairs={{0,4},{1,5},{2,6},{3,7},{4,0},{5,1},{6,2},{7,3},{8,12},{9,13},{10,... | collective-permute-start | bytes 393224 | tf_op jit(solution)/shard_map/ppermute | solution.py:385
  26.6 15.3 %collective-permute-start.15 = (bf16[256,512]{1,0:T(8,128)(2,1)S(1)}, bf16[256,512]{1,0:T(8,128)(2,1)S(1)}, u32[]{:S(2)}, u32[]{:S(2)}) collective-permute-start(bf16[256,512]{1,0:T(8,128)(2,1)S(1)} %shard_map.116.refs_0_), channel_id=1, source_target_pairs={{0,2},{1,3},{2,0},{3,1},{4,6},{5,7},{6,4},{7,5},{8,10},{9,11},{10,... | collective-permute-start | bytes 786440 | tf_op jit(solution)/shard_map/ppermute | solution.py:385
  28.4 4.0 %collective-permute-start.12 = (bf16[128,512]{1,0:T(8,128)(2,1)S(1)}, bf16[128,512]{1,0:T(8,128)(2,1)S(1)}, u32[]{:S(2)}, u32[]{:S(2)}) collective-permute-start(bf16[128,512]{1,0:T(8,128)(2,1)S(1)} %collective-permute-done.4.refs_2_), channel_id=1, source_target_pairs={{0,1},{1,0},{2,3},{3,2},{4,5},{5,4},{6,7},{7,6},{8,9},{9,8},{10,11... | collective-permute-start | bytes 393224 | tf_op jit(solution)/shard_map/ppermute | solution.py:385
  28.4 10.3 %collective-permute-start.5 = (bf16[128,512]{1,0:T(8,128)(2,1)S(1)}, bf16[128,512]{1,0:T(8,128)(2,1)S(1)}, u32[]{:S(2)}, u32[]{:S(2)}) collective-permute-start(bf16[128,512]{1,0:T(8,128)(2,1)S(1)} %collective-permute-done.4.refs_2_), channel_id=1, source_target_pairs={{0,2},{1,3},{2,0},{3,1},{4,6},{5,7},{6,4},{7,5},{8,10},{9,11},{10,... | collective-permute-start | bytes 393224 | tf_op jit(solution)/shard_map/ppermute | solution.py:385
  30.9 9.5 %collective-permute-start.13 = (bf16[128,512]{1,0:T(8,128)(2,1)S(1)}, bf16[128,512]{1,0:T(8,128)(2,1)S(1)}, u32[]{:S(2)}, u32[]{:S(2)}) collective-permute-start(bf16[128,512]{1,0:T(8,128)(2,1)S(1)} %collective-permute-done.7.refs_3_), channel_id=1, source_target_pairs={{0,1},{1,0},{2,3},{3,2},{4,5},{5,4},{6,7},{7,6},{8,9},{9,8},{10,11... | collective-permute-start | bytes 393224 | tf_op jit(solution)/shard_map/ppermute | solution.py:385
  30.9 15.2 %collective-permute-start.10 = (bf16[256,512]{1,0:T(8,128)(2,1)S(1)}, bf16[256,512]{1,0:T(8,128)(2,1)S(1)}, u32[]{:S(2)}, u32[]{:S(2)}) collective-permute-start(bf16[256,512]{1,0:T(8,128)(2,1)S(1)} %get-tuple-element.31.refs_0_), channel_id=1, source_target_pairs={{0,2},{1,3},{2,0},{3,1},{4,6},{5,7},{6,4},{7,5},{8,10},{9,11},{10,... | collective-permute-start | bytes 786440 | tf_op jit(solution)/shard_map/ppermute | solution.py:385
  32.4 15.4 %collective-permute-start.14 = (bf16[256,512]{1,0:T(8,128)(2,1)S(1)}, bf16[256,512]{1,0:T(8,128)(2,1)S(1)}, u32[]{:S(2)}, u32[]{:S(2)}) collective-permute-start(bf16[256,512]{1,0:T(8,128)(2,1)S(1)} %get-tuple-element.31.refs_0_), channel_id=1, source_target_pairs={{0,1},{1,0},{2,3},{3,2},{4,5},{5,4},{6,7},{7,6},{8,9},{9,8},{10,11... | collective-permute-start | bytes 786440 | tf_op jit(solution)/shard_map/ppermute | solution.py:385
  38.7 9.1 %collective-permute-start.19 = (bf16[256,512]{1,0:T(8,128)(2,1)S(1)}, bf16[256,512]{1,0:T(8,128)(2,1)S(1)}, u32[]{:S(2)}, u32[]{:S(2)}) collective-permute-start(bf16[256,512]{1,0:T(8,128)(2,1)S(1)} %shard_map.116.refs_0_), channel_id=1, source_target_pairs={{0,4},{1,5},{2,6},{3,7},{4,0},{5,1},{6,2},{7,3},{8,12},{9,13},{10,... | collective-permute-start | bytes 786440 | tf_op jit(solution)/shard_map/ppermute | solution.py:385
  40.4 5.7 %collective-permute-start.8 = (bf16[128,512]{1,0:T(8,128)(2,1)S(1)}, bf16[128,512]{1,0:T(8,128)(2,1)S(1)}, u32[]{:S(2)}, u32[]{:S(2)}) collective-permute-start(bf16[128,512]{1,0:T(8,128)(2,1)S(1)} %collective-permute-done.7.refs_3_), channel_id=1, source_target_pairs={{0,2},{1,3},{2,0},{3,1},{4,6},{5,7},{6,4},{7,5},{8,10},{9,11},{10,... | collective-permute-start | bytes 393224 | tf_op jit(solution)/shard_map/ppermute | solution.py:385
  41.9 8.7 %collective-permute-start.16 = (bf16[256,512]{1,0:T(8,128)(2,1)S(1)}, bf16[256,512]{1,0:T(8,128)(2,1)S(1)}, u32[]{:S(2)}, u32[]{:S(2)}) collective-permute-start(bf16[256,512]{1,0:T(8,128)(2,1)S(1)} %collective-permute-done.15.refs_0_), channel_id=1, source_target_pairs={{0,4},{1,5},{2,6},{3,7},{4,0},{5,1},{6,2},{7,3},{8,12},{9,13},{10,... | collective-permute-start | bytes 786440 | tf_op jit(solution)/shard_map/ppermute | solution.py:385
  46.1 4.5 %collective-permute-start.21 = (bf16[256,512]{1,0:T(8,128)(2,1)S(1)}, bf16[256,512]{1,0:T(8,128)(2,1)S(1)}, u32[]{:S(2)}, u32[]{:S(2)}) collective-permute-start(bf16[256,512]{1,0:T(8,128)(2,1)S(1)} %shard_map.116.refs_0_), channel_id=1, source_target_pairs={{0,1},{1,0},{2,3},{3,2},{4,5},{5,4},{6,7},{7,6},{8,9},{9,8},{10,11... | collective-permute-start | bytes 786440 | tf_op jit(solution)/shard_map/ppermute | solution.py:385
  46.1 5.0 %collective-permute-start.11 = (bf16[256,512]{1,0:T(8,128)(2,1)S(1)}, bf16[256,512]{1,0:T(8,128)(2,1)S(1)}, u32[]{:S(2)}, u32[]{:S(2)}) collective-permute-start(bf16[256,512]{1,0:T(8,128)(2,1)S(1)} %collective-permute-done.10.refs_0_), channel_id=1, source_target_pairs={{0,1},{1,0},{2,3},{3,2},{4,5},{5,4},{6,7},{7,6},{8,9},{9,8},{10,11... | collective-permute-start | bytes 786440 | tf_op jit(solution)/shard_map/ppermute | solution.py:385
  47.8 5.3 %collective-permute-start.20 = (bf16[256,512]{1,0:T(8,128)(2,1)S(1)}, bf16[256,512]{1,0:T(8,128)(2,1)S(1)}, u32[]{:S(2)}, u32[]{:S(2)}) collective-permute-start(bf16[256,512]{1,0:T(8,128)(2,1)S(1)} %collective-permute-done.19.refs_2_), channel_id=1, source_target_pairs={{0,1},{1,0},{2,3},{3,2},{4,5},{5,4},{6,7},{7,6},{8,9},{9,8},{10,11... | collective-permute-start | bytes 786440 | tf_op jit(solution)/shard_map/ppermute | solution.py:385
  47.8 5.3 %collective-permute-start.18 = (bf16[256,512]{1,0:T(8,128)(2,1)S(1)}, bf16[256,512]{1,0:T(8,128)(2,1)S(1)}, u32[]{:S(2)}, u32[]{:S(2)}) collective-permute-start(bf16[256,512]{1,0:T(8,128)(2,1)S(1)} %collective-permute-done.15.refs_0_), channel_id=1, source_target_pairs={{0,1},{1,0},{2,3},{3,2},{4,5},{5,4},{6,7},{7,6},{8,9},{9,8},{10,11... | collective-permute-start | bytes 786440 | tf_op jit(solution)/shard_map/ppermute | solution.py:385
  50.6 3.3 %collective-permute-start.17 = (bf16[256,512]{1,0:T(8,128)(2,1)S(1)}, bf16[256,512]{1,0:T(8,128)(2,1)S(1)}, u32[]{:S(2)}, u32[]{:S(2)}) collective-permute-start(bf16[256,512]{1,0:T(8,128)(2,1)S(1)} %collective-permute-done.16.refs_0_), channel_id=1, source_target_pairs={{0,1},{1,0},{2,3},{3,2},{4,5},{5,4},{6,7},{7,6},{8,9},{9,8},{10,11... | collective-permute-start | bytes 786440 | tf_op jit(solution)/shard_map/ppermute | solution.py:385
  50.6 3.7 %collective-permute-start.6 = (bf16[128,512]{1,0:T(8,128)(2,1)S(1)}, bf16[128,512]{1,0:T(8,128)(2,1)S(1)}, u32[]{:S(2)}, u32[]{:S(2)}) collective-permute-start(bf16[128,512]{1,0:T(8,128)(2,1)S(1)} %collective-permute-done.5.refs_0_), channel_id=1, source_target_pairs={{0,1},{1,0},{2,3},{3,2},{4,5},{5,4},{6,7},{7,6},{8,9},{9,8},{10,11... | collective-permute-start | bytes 393224 | tf_op jit(solution)/shard_map/ppermute | solution.py:385
  51.1 3.2 %collective-permute-start.9 = (bf16[128,512]{1,0:T(8,128)(2,1)S(1)}, bf16[128,512]{1,0:T(8,128)(2,1)S(1)}, u32[]{:S(2)}, u32[]{:S(2)}) collective-permute-start(bf16[128,512]{1,0:T(8,128)(2,1)S(1)} %collective-permute-done.8.refs_1_), channel_id=1, source_target_pairs={{0,1},{1,0},{2,3},{3,2},{4,5},{5,4},{6,7},{7,6},{8,9},{9,8},{10,11... | collective-permute-start | bytes 393224 | tf_op jit(solution)/shard_map/ppermute | solution.py:385
